TPU v7x, 32 devices: a whole 2x2x4 slice. The times are simulated.
32 devices in a mesh: region: 4 (over x, core), domain: 8 (over z, y).
Axes of the slice: x: 2, y: 2, z: 4, core: 2. Of those that a mesh axis runs over, the one named last changes fastest.
Arguments:
- midpoints: float32 [3, 16384], P(None, ('region', 'domain')), may hold values from 0 to 1, as said below
- line_vectors: float32 [3, 16384], P(None, ('region', 'domain')), may hold values from -0.09375 to 0.09375
- burgers: float32 [3, 16384], P(None, ('region', 'domain')), may hold values from -4 to 4
- destination: int32 [16384, 1], P(('region', 'domain')), may hold values from 0 to 7; in each aligned block of 512 rows (0 to 511, 512 to 1023, ...) at most 128 rows name the same one
- node_ids: int32 [2, 16384], P(None, ('region', 'domain')), may hold values from 0 to 2047
- cell_ids: int32 [16384], P(('region', 'domain')), may hold values from 0 to 127, as said below
- cell_centers: float32 [3, 512], replicated, may hold values from 0 to 1, as said below
Outputs:
- slot_traction: float32 [3, 32768], P(None, ('region', 'domain'))
- nodal_force: float32 [3, 8192], P(None, ('region', 'domain'))
Inputs may be any that keep to these rules, and one draw needn't show every extreme that they name: `destination`: among the rows of one device, no domain is named by more than 128 rows, a bound that some block reaches. `cell_ids`: region r is the slab of x from r / 4 to (r + 1) / 4 of the unit cube; its 128 cells are the boxes of a 2 x 4 x (16) grid in that slab, numbered with the last grid index fastest. `cell_centers`: each cell's center lies within its box, within a quarter of the box's width of the box's middle along each dimension. `midpoints`: each segment's midpoint lies within its cell's box.
All inputs are finite; a program needn't handle non-finite values.
Results may differ from a plain program's by a relative error of at most 0.0003.
Values sent between devices are 32-bit elements; how exact they have to be, the bound alone decides.
No kernel may reach another device: no remote copies, remote signals or barrier semaphores. Data moves between devices by JAX's collectives and lax.ppermute only.
A program may use at most 64 MiB of HBM per device.

v0:
```python
import jax
import jax.numpy as jnp
from jax import lax
from jax.sharding import PartitionSpec as P

CELLS_REG = 128
CORE2 = 0.01
EXACT = lax.Precision.HIGHEST


def product(left, right):
    return jnp.dot(left, right, precision=EXACT, preferred_element_type=jnp.float32)


def source_terms(m, l, b):
    count = m.shape[1]
    outer = (b[:, None, :] * l[None, :, :]).reshape(9, count)
    q = jnp.cross(b, l, axis=0)
    qm = (q[:, None, :] * m[None, :, :]).reshape(9, count)
    return (outer, jnp.concatenate([qm, q], axis=0))


def pair_block(m, outer, second, targets):
    r2 = (targets[0][None, :] - m[0][:, None]) ** 2
    r2 = r2 + (targets[1][None, :] - m[1][:, None]) ** 2
    r2 = r2 + (targets[2][None, :] - m[2][:, None]) ** 2
    g1 = 1.0 / jnp.sqrt(r2 + CORE2)
    g3 = g1 * g1 * g1
    first = product(outer, g1)
    other = product(second, g3)
    cross_part = (other[9:12][:, None, :] * targets[None, :, :]).reshape(9, targets.shape[1])
    return first + cross_part - other[0:9]


def moment_terms(m, l, b, centers):
    count = m.shape[1]
    outer = (b[:, None, :] * l[None, :, :]).reshape(9, count)
    offset = m - centers
    dipole = (outer[:, None, :] * offset[None, :, :]).reshape(27, count)
    q = jnp.cross(b, l, axis=0)
    return jnp.concatenate([outer, dipole, q], axis=0)


def far_field(moments, centers, region_centers, region, cells_reg):
    total = centers.shape[1]
    diffs = [region_centers[a][None, :] - centers[a][:, None] for a in range(3)]
    r2 = diffs[0] ** 2 + diffs[1] ** 2 + diffs[2] ** 2
    keep = (jnp.arange(total, dtype=jnp.int32) // cells_reg != region).astype(jnp.float32)
    g1 = keep[:, None] / jnp.sqrt(r2 + CORE2)
    g3 = g1 * g1 * g1
    field = product(moments[0:9], g1)
    pulls = []
    for axis_a in range(3):
        weighted = diffs[axis_a] * g3
        field = field + product(moments[9 + axis_a : 36 : 3], weighted)
        pulls.append(product(moments[36:39], weighted))
    nterm = jnp.stack(pulls, axis=1).reshape(9, region_centers.shape[1])
    return field + nterm


def traction(stress, b):
    count = stress.shape[1]
    sigma = stress.reshape(3, 3, count)
    sym = 0.5 * (sigma + jnp.transpose(sigma, (1, 0, 2)))
    return jnp.sum(sym * b[None, :, :], axis=1)


def fold_blocks(total_stress, rows, block_fn):
    width = rows.shape[1]
    if width <= 1024 or width % 512 != 0:
        return total_stress + block_fn(rows)
    split = jnp.transpose(rows.reshape(rows.shape[0], width // 512, 512), (1, 0, 2))

    def step(carry, part):
        return (carry + block_fn(part), None)

    result, _ = lax.scan(step, total_stress, split)
    return result


def body(midpoints, line_vectors, burgers, destination, node_ids, cell_ids, cell_centers):
    count = midpoints.shape[1]
    domains = lax.axis_size("domain")
    capacity = 2 * count // domains
    slots = 2 * count
    region = lax.axis_index("region")
    region_centers = lax.dynamic_slice_in_dim(cell_centers, region * CELLS_REG, CELLS_REG, 1)
    cell_table = (jnp.arange(CELLS_REG, dtype=jnp.int32)[:, None] == cell_ids[None, :]).astype(
        jnp.float32
    )
    seg_centers = product(region_centers, cell_table)
    feats = moment_terms(midpoints, line_vectors, burgers, seg_centers)
    partial_value = product(feats, cell_table.T)
    summed = lax.psum(partial_value, "domain")
    moments = lax.all_gather(summed, "region", axis=1, tiled=True)
    far = far_field(moments, cell_centers, region_centers, region, CELLS_REG)

    def near_stress(targets):
        empty = jnp.zeros((9, targets.shape[1]), jnp.float32)
        outer, second = source_terms(midpoints, line_vectors, burgers)
        payload = jnp.concatenate([midpoints, outer, second], axis=0)

        def expanded_block(rows):
            return pair_block(rows[0:3], rows[3:12], rows[12:24], targets)

        return fold_blocks(
            empty, lax.all_gather(payload, "domain", axis=1, tiled=True), expanded_block
        )

    dest = destination[:, 0]
    hot = (dest[:, None] == jnp.arange(domains, dtype=jnp.int32)[None, :]).astype(jnp.int32)
    rank = jnp.sum(jnp.cumsum(hot, axis=0) * hot, axis=1) - 1
    slot = dest * capacity + rank
    stress = near_stress(midpoints) + product(far, cell_table)
    force = traction(stress, burgers)
    outgoing = jnp.zeros((3, slots), jnp.float32).at[:, slot].set(force)
    slot_traction = lax.all_to_all(outgoing, "domain", split_axis=1, concat_axis=1, tiled=True)
    half = 0.5 * force
    node_partial = jnp.zeros((3, count // 2 * domains), jnp.float32)
    node_partial = node_partial.at[:, node_ids[0]].add(half).at[:, node_ids[1]].add(half)
    nodal_force = lax.psum_scatter(node_partial, "domain", scatter_dimension=1, tiled=True)
    return (slot_traction, nodal_force)


def solution(mesh):
    in_specs = (
        P(None, ("region", "domain")),
        P(None, ("region", "domain")),
        P(None, ("region", "domain")),
        P(("region", "domain"), None),
        P(None, ("region", "domain")),
        P(("region", "domain")),
        P(),
    )
    out_specs = (P(None, ("region", "domain")), P(None, ("region", "domain")))
    return jax.shard_map(body, mesh=mesh, in_specs=in_specs, out_specs=out_specs, check_vma=False)
```

profile of v0, /device:TPU:0, one launch (start us, length us, event | category | flops | bytes accessed | tf_op | source)
XLA Modules:
  0.0 186.8 jit_solution(9238915904574163798)
XLA Ops:
  9.8 38.9 %psum.7 = f32[39,128]{1,0:T(8,128)S(1)} all-reduce(f32[39,128]{1,0:T(8,128)S(1)} %fusion.27), channel_id=1, replica_groups=mesh['region'=4,'domain'=8] {'domain'}, use_global_device_ids=true, to_apply=%region_5.7 | all-reduce | flops 4992 | bytes 39936 | tf_op jit(solution)/shard_map/psum | solution.py:94
  48.7 5.3 %all_gather.7 = f32[39,512]{1,0:T(8,128)S(1)} all-gather(f32[39,128]{1,0:T(8,128)S(1)} %psum.7), channel_id=1, replica_groups=mesh['region'=4,'domain'=8] {'region'}, dimensions={1}, use_global_device_ids=true | all-gather | bytes 99840 | tf_op jit(solution)/shard_map/all_gather | solution.py:95
  56.4 31.0 %all_gather.6 = f32[24,4096]{1,0:T(8,128)S(1)} all-gather(f32[24,512]{1,0:T(8,128)S(1)} %maximum_maximum_fusion), channel_id=1, replica_groups=mesh['region'=4,'domain'=8] {'domain'}, dimensions={1}, use_global_device_ids=true | all-gather | bytes 442368 | tf_op jit(solution)/shard_map/all_gather | solution.py:107
  87.6 18.2 %while.11 = (s32[]{:T(128)}, f32[9,512]{1,0:T(8,128)S(1)}, f32[8,24,512]{2,0,1:T(8,128)S(1)}, f32[3,512]{1,0:T(4,128)S(1)}, s32[]{:T(128)}, /*index=5*/s32[]{:T(128)}, s32[]{}, s32[]{}, s32[]{}, s32[]{}) while((s32[]{:T(128)}, f32[9,512]{1,0:T(8,128)S(1)}, f32[8,24,512]{2,0,1:T(8,128)S(1)}, f32[3,512]{1,0:T(4,128)S(1)}, s32[]{:T(128)}, ...), condition=%wide.region_4.6_spmd.clone, body=%wide.region_3.5_spmd.clone.sunk | while | flops 71326208 | bytes 356539 | solution.py:77
  87.6 1.1 fusion.96
  88.8 1.0 fusion.97
  89.9 1.1 fusion.96
  92.2 1.1 fusion.96
  93.4 1.0 fusion.97
  94.5 1.1 fusion.96
  95.6 1.0 fusion.97
  96.7 1.1 fusion.96
  97.9 1.0 fusion.97
  99.0 1.1 fusion.96
  101.3 1.1 fusion.96
  103.6 1.1 fusion.96
  104.7 1.0 fusion.97
  108.4 2.5 %scatter_custom_fusion.1 = f32[3,2048]{0,1:T(8,128)S(1)} fusion(s32[512]{0:T(512)S(1)} %bitcast.138, f32[512,3]{1,0:T(8,128)S(1)} %copy.28, f32[]{:T(128)} %constant.24.clone.1), kind=kCustom, calls=%fused_computation.42 | custom fusion | flops 1536 | bytes 24580 | tf_op jit(solution)/shard_map/scatter-add | solution.py:120
  110.9 3.7 %scatter_fusion = f32[3,2048]{0,1:T(8,128)S(1)} fusion(f32[3,2048]{0,1:T(8,128)S(1)} %scatter_custom_fusion.1, s32[512]{0:T(512)S(1)} %bitcast.114, f32[512,3]{1,0:T(8,128)S(1)} %copy.28), kind=kCustom, calls=%fused_computation.2 | custom fusion | flops 1536 | bytes 20480 | tf_op jit(solution)/shard_map/scatter-add | solution.py:120
  115.6 1.1 reduce-window.6
  117.3 1.8 scatter_custom_fusion
  119.3 9.0 %all_to_all.12 = f32[3,8,128]{2,0,1:T(4,128)S(1)} all-to-all(f32[3,8,128]{2,0,1:T(4,128)S(1)} %copy.27), channel_id=1, replica_groups=mesh['region'=4,'domain'=8] {'domain'}, dimensions={1} | all-to-all | bytes 24576 | tf_op jit(solution)/shard_map/all_to_all | solution.py:117
  128.4 49.4 %reduce-scatter.2.cloned.1.call-done = f32[3,256]{0,1:T(8,128)} async-done(((f32[3,2048]{0,1:T(8,128)}), f32[3,256]{0,1:T(8,128)}) %reduce-scatter.2.cloned.1.call-update) | async-done | bytes 3088 | tf_op jit(solution)/shard_map/reduce_scatter | solution.py:121
  177.7 1.6 copy.30
  (124 shorter events, 13.9 us)
Async XLA Ops:
  7.2 0.7 copy-start.5
  7.2 170.6 %reduce-scatter.2.cloned.1.call-start = ((), (), s32[]{:S(2)}) async-start(), calls=%async_computation.2 | async-start | bytes 1179648 | tf_op jit(solution)/shard_map/reduce_scatter | solution.py:121
  7.9 0.7 copy-start.2
  7.9 0.7 copy-start.3
  8.6 0.7 copy-start.1
  8.6 0.7 copy-start.7
  107.7 0.7 copy-start.6
  114.6 1.0 copy-start
  114.6 1.0 copy-start.4
Sparse Core Ops, SparseCore 0:
  115.7 61.9 reduce-scatter.1
where the time goes:
time: 187 us
  blocking collectives  84.1 us (45%)
  waiting for transfers between devices  49.4 us (26%)
  matrix products  21.4 us (11%)
  between operations  14.3 us (8%)
  local copies, waits for them, and re-layouts  9.35 us (5%)
  other arithmetic  7.69 us (4%)
    reduce_scatter x1, waiting for transfers between devices, body(): lax.psum_scatter(node_partial, 'domain', scatter_dimension=1, tiled=True)  49.4 us
    psum x1, blocking collectives, body(): summed = lax.psum(partial_value, 'domain')  38.9 us
    all_gather x1, blocking collectives, near_stress(): lax.all_gather(payload, 'domain', axis=1, tiled=True)  31 us
    dot_general x26, matrix products, product(): jnp.dot(left, right, precision=EXACT, preferred_element_type=jnp.float32)  21.4 us
    all_to_all x1, blocking collectives, body(): lax.all_to_all(outgoing, 'domain', split_axis=1, concat_axis=1, tiled=True)  9.02 us
    scatter-add x2, other arithmetic, body(): node_partial.at[:, node_ids[0]].add(half).at[:, node_ids[1]].add(half)  6.19 us
    unnamed x19, local copies, waits for them, and re-layouts  5.89 us
    all_gather x1, blocking collectives, body(): moments = lax.all_gather(summed, 'region', axis=1, tiled=True)  5.27 us
  transfers between devices with their start and end apart: 1, of which 1 were waited for; matrix products, arithmetic and copies ran while one was open for 2% of the time, Pallas kernels for 0%

commit v1 on v0

--- a/solution.py
+++ b/solution.py
@@ -91,7 +91,9 @@
     seg_centers = product(region_centers, cell_table)
     feats = moment_terms(midpoints, line_vectors, burgers, seg_centers)
     partial_value = product(feats, cell_table.T)
-    summed = lax.psum(partial_value, "domain")
+    summed = partial_value
+    for hop in (1, 2, 4):
+        summed = summed + lax.ppermute(summed, "domain", [(dev, dev ^ hop) for dev in range(8)])
     moments = lax.all_gather(summed, "region", axis=1, tiled=True)
     far = far_field(moments, cell_centers, region_centers, region, CELLS_REG)
 

time: 187 us -> 165 us (0.88)
  blocking collectives: 84.1 us -> 47.7 us
  waiting for transfers between devices: 49.4 us -> 59.8 us
  starting transfers between devices: 0.04 us -> 3.17 us
    psum x1 -> x0, blocking collectives: 38.9 us -> none  [body(): summed = lax.psum(partial_value, 'domain')]
    ppermute x0 -> x3, waiting for transfers between devices: none -> 8.42 us  [body(): lax.ppermute(summed, 'domain', [(dev, dev ^ hop) for dev in range(8)])]
    ppermute x0 -> x3, starting transfers between devices: none -> 3.13 us  [body(): lax.ppermute(summed, 'domain', [(dev, dev ^ hop) for dev in range(8)])]
    reduce_scatter x1, waiting for transfers between devices: 49.4 us -> 51.4 us  [body(): lax.psum_scatter(node_partial, 'domain', scatter_dimension=1, tiled=True)]
  transfers between devices with their start and end apart: 1 -> 4, of which waited for: 1 -> 3; matrix products, arithmetic and copies ran while one was open for 2% -> 13% of each run, Pallas kernels for 0% -> 0%
where the time goes in v1:
time: 165 us
  waiting for transfers between devices  59.8 us (36%)
  blocking collectives  47.7 us (29%)
  matrix products  21.4 us (13%)
  between operations  14.4 us (9%)
  local copies, waits for them, and re-layouts  9.49 us (6%)
  other arithmetic  8.41 us (5%)
  starting transfers between devices  3.17 us (2%)
    reduce_scatter x1, waiting for transfers between devices, body(): lax.psum_scatter(node_partial, 'domain', scatter_dimension=1, tiled=True)  51.4 us
    all_gather x1, blocking collectives, near_stress(): lax.all_gather(payload, 'domain', axis=1, tiled=True)  31.6 us
    dot_general x26, matrix products, product(): jnp.dot(left, right, precision=EXACT, preferred_element_type=jnp.float32)  21.4 us
    all_to_all x1, blocking collectives, body(): lax.all_to_all(outgoing, 'domain', split_axis=1, concat_axis=1, tiled=True)  10.9 us
    ppermute x3, waiting for transfers between devices, body(): lax.ppermute(summed, 'domain', [(dev, dev ^ hop) for dev in range(8)])  8.42 us
    scatter-add x2, other arithmetic, body(): node_partial.at[:, node_ids[0]].add(half).at[:, node_ids[1]].add(half)  6.2 us
    unnamed x19, local copies, waits for them, and re-layouts  6.05 us
    all_gather x1, blocking collectives, body(): moments = lax.all_gather(summed, 'region', axis=1, tiled=True)  5.27 us
  transfers between devices with their start and end apart: 4, of which 3 were waited for; matrix products, arithmetic and copies ran while one was open for 13% of the time, Pallas kernels for 0%

profile of v1, /device:TPU:0, one launch (start us, length us, event | category | flops | bytes accessed | tf_op | source)
XLA Modules:
  0.0 164.8 jit_solution(14092381199891915226)
XLA Ops:
  11.1 3.1 %collective-permute-start = (f32[39,128]{1,0:T(8,128)S(1)}, f32[39,128]{1,0:T(8,128)S(1)}, u32[]{:S(2)}, u32[]{:S(2)}) collective-permute-start(f32[39,128]{1,0:T(8,128)S(1)} %fusion.29), channel_id=1, source_target_pairs={{0,1},{1,0},{2,3},{3,2},{4,5},{5,4},{6,7},{7,6},{8,9},{9,8},{10,11... | collective-permute-start | bytes 59912 | tf_op jit(solution)/shard_map/ppermute | solution.py:96
  14.3 31.6 %all_gather.6 = f32[24,4096]{1,0:T(8,128)S(1)} all-gather(f32[24,512]{1,0:T(8,128)S(1)} %maximum_maximum_fusion), channel_id=1, replica_groups=mesh['region'=4,'domain'=8] {'domain'}, dimensions={1}, use_global_device_ids=true | all-gather | bytes 442368 | tf_op jit(solution)/shard_map/all_gather | solution.py:109
  46.2 18.2 %while.11 = (s32[]{:T(128)}, f32[9,512]{1,0:T(8,128)S(1)}, f32[8,24,512]{2,0,1:T(8,128)S(1)}, f32[3,512]{1,0:T(4,128)S(1)}, s32[]{:T(128)}, /*index=5*/s32[]{:T(128)}, s32[]{}, s32[]{}, s32[]{}, s32[]{}) while((s32[]{:T(128)}, f32[9,512]{1,0:T(8,128)S(1)}, f32[8,24,512]{2,0,1:T(8,128)S(1)}, f32[3,512]{1,0:T(4,128)S(1)}, s32[]{:T(128)}, ...), condition=%wide.region_4.6_spmd.clone, body=%wide.region_3.5_spmd.clone.sunk | while | flops 71326208 | bytes 356539 | solution.py:77
  46.3 1.1 fusion.100
  47.4 1.0 fusion.101
  48.5 1.1 fusion.100
  49.7 1.0 fusion.101
  50.8 1.1 fusion.100
  52.0 1.0 fusion.101
  53.1 1.1 fusion.100
  55.4 1.1 fusion.100
  57.6 1.1 fusion.100
  59.9 1.1 fusion.100
  62.2 1.1 fusion.100
  64.4 1.1 reduce-window.6
  66.0 3.8 %collective-permute-done.1 = f32[39,128]{1,0:T(8,128)S(1)} collective-permute-done((f32[39,128]{1,0:T(8,128)S(1)}, f32[39,128]{1,0:T(8,128)S(1)}, u32[]{:S(2)}, u32[]{:S(2)}) %collective-permute-start.1) | collective-permute-done | bytes 20000 | tf_op jit(solution)/shard_map/ppermute | solution.py:96
  69.8 4.7 %collective-permute-done.2 = f32[39,128]{1,0:T(8,128)S(1)} collective-permute-done((f32[39,128]{1,0:T(8,128)S(1)}, f32[39,128]{1,0:T(8,128)S(1)}, u32[]{:S(2)}, u32[]{:S(2)}) %collective-permute-start.2) | collective-permute-done | bytes 20000 | tf_op jit(solution)/shard_map/ppermute | solution.py:96
  74.5 5.3 %all_gather.7 = f32[39,512]{1,0:T(8,128)S(1)} all-gather(f32[39,128]{1,0:T(8,128)S(1)} %add.117), channel_id=1, replica_groups=mesh['region'=4,'domain'=8] {'region'}, dimensions={1}, use_global_device_ids=true | all-gather | bytes 99840 | tf_op jit(solution)/shard_map/all_gather | solution.py:97
  84.1 2.5 %scatter_custom_fusion.1 = f32[3,2048]{0,1:T(8,128)S(1)} fusion(s32[512]{0:T(512)S(1)} %bitcast.138, f32[512,3]{1,0:T(8,128)S(1)} %copy.28, f32[]{:T(128)} %constant.24.clone.1), kind=kCustom, calls=%fused_computation.42 | custom fusion | flops 1536 | bytes 24580 | tf_op jit(solution)/shard_map/scatter-add | solution.py:122
  86.7 3.7 %scatter_fusion = f32[3,2048]{0,1:T(8,128)S(1)} fusion(f32[3,2048]{0,1:T(8,128)S(1)} %scatter_custom_fusion.1, s32[512]{0:T(512)S(1)} %bitcast.114, f32[512,3]{1,0:T(8,128)S(1)} %copy.28), kind=kCustom, calls=%fused_computation.2 | custom fusion | flops 1536 | bytes 20480 | tf_op jit(solution)/shard_map/scatter-add | solution.py:122
  91.5 1.8 %scatter_custom_fusion = f32[3,1024]{0,1:T(8,128)S(1)} fusion(s32[512]{0:T(512)S(1)} %bitcast.116, f32[512,3]{1,0:T(8,128)S(1)} %copy.26, f32[]{:T(128)} %constant.24.clone.1), kind=kCustom, calls=%fused_computation.58 | custom fusion | bytes 12292 | tf_op jit(solution)/shard_map/scatter | solution.py:118
  93.6 10.9 %all_to_all.12 = f32[3,8,128]{2,0,1:T(4,128)S(1)} all-to-all(f32[3,8,128]{2,0,1:T(4,128)S(1)} %copy.27), channel_id=1, replica_groups=mesh['region'=4,'domain'=8] {'domain'}, dimensions={1} | all-to-all | bytes 24576 | tf_op jit(solution)/shard_map/all_to_all | solution.py:119
  104.4 51.4 %reduce-scatter.2.cloned.1.call-done = f32[3,256]{0,1:T(8,128)} async-done(((f32[3,2048]{0,1:T(8,128)}), f32[3,256]{0,1:T(8,128)}) %reduce-scatter.2.cloned.1.call-update) | async-done | bytes 3088 | tf_op jit(solution)/shard_map/reduce_scatter | solution.py:123
  155.8 1.6 copy.30
  (132 shorter events, 16.8 us)
Async XLA Ops:
  7.2 0.7 copy-start.2
  7.2 148.6 %reduce-scatter.2.cloned.1.call-start = ((), (), s32[]{:S(2)}) async-start(), calls=%async_computation.2 | async-start | bytes 1179648 | tf_op jit(solution)/shard_map/reduce_scatter | solution.py:123
  8.6 0.7 copy-start.5
  8.6 0.7 copy-start.1
  9.3 0.7 copy-start.7
  10.2 0.7 copy-start.3
  11.1 54.8 %collective-permute-start = (f32[39,128]{1,0:T(8,128)S(1)}, f32[39,128]{1,0:T(8,128)S(1)}, u32[]{:S(2)}, u32[]{:S(2)}) collective-permute-start(f32[39,128]{1,0:T(8,128)S(1)} %fusion.29), channel_id=1, source_target_pairs={{0,1},{1,0},{2,3},{3,2},{4,5},{5,4},{6,7},{7,6},{8,9},{9,8},{10,11... | collective-permute-start | bytes 59912 | tf_op jit(solution)/shard_map/ppermute | solution.py:96
  46.2 18.2 %copy-start.6 = (s32[2,512]{1,0:T(2,128)S(1)}, s32[2,512]{1,0:T(2,128)}, u32[]{:S(2)}) copy-start(s32[2,512]{1,0:T(2,128)} %param.15) | copy-start | bytes 12292
  46.2 18.2 %copy-start.4 = (s32[512,1]{0,1:T(1,128)S(1)}, s32[512,1]{0,1:T(1,128)}, u32[]{:S(2)}) copy-start(s32[512,1]{0,1:T(1,128)} %param.14) | copy-start | bytes 6148
  66.0 3.8 %collective-permute-start.1 = (f32[39,128]{1,0:T(8,128)S(1)}, f32[39,128]{1,0:T(8,128)S(1)}, u32[]{:S(2)}, u32[]{:S(2)}) collective-permute-start(f32[39,128]{1,0:T(8,128)S(1)} %add.115), channel_id=1, source_target_pairs={{0,2},{1,3},{2,0},{3,1},{4,6},{5,7},{6,4},{7,5},{8,10},{9,11},{10,... | collective-permute-start | bytes 59912 | tf_op jit(solution)/shard_map/ppermute | solution.py:96
  69.8 4.7 %collective-permute-start.2 = (f32[39,128]{1,0:T(8,128)S(1)}, f32[39,128]{1,0:T(8,128)S(1)}, u32[]{:S(2)}, u32[]{:S(2)}) collective-permute-start(f32[39,128]{1,0:T(8,128)S(1)} %add.116), channel_id=1, source_target_pairs={{0,4},{1,5},{2,6},{3,7},{4,0},{5,1},{6,2},{7,3},{8,12},{9,13},{10,... | collective-permute-start | bytes 59912 | tf_op jit(solution)/shard_map/ppermute | solution.py:96
  90.4 1.0 copy-start
Sparse Core Ops, SparseCore 0:
  91.5 64.2 reduce-scatter.1
